TPU v7x, 16 devices: a 4x2x1 block of a 4x4x8 slice. The times are simulated.
16 devices in a mesh: rep: 4 (over y, z, core), dp: 4 (over x).
Axes of the slice: x: 4, y: 2, z: 1, core: 2. Of those that a mesh axis runs over, the one named last changes fastest.
The devices are a block of a 4x4x8 slice.
Arguments:
- g_w_gate: bfloat16 [16, 2, 896, 2304], P(('rep', 'dp')), parts along dimension 0
- g_w_up: bfloat16 [16, 2, 896, 2304], P(('rep', 'dp')), parts along dimension 0
- g_w_down: bfloat16 [16, 2, 2304, 896], P(('rep', 'dp')), parts along dimension 0
- w_gate: bfloat16 [2, 896, 2304], replicated
- w_up: bfloat16 [2, 896, 2304], replicated
- w_down: bfloat16 [2, 2304, 896], replicated
- m_w_gate: float32 [2, 896, 2304], P(None, 'dp')
- m_w_up: float32 [2, 896, 2304], P(None, 'dp')
- m_w_down: float32 [2, 2304, 896], P(None, 'dp')
- v_w_gate: float32 [2, 896, 2304], P(None, 'dp')
- v_w_up: float32 [2, 896, 2304], P(None, 'dp')
- v_w_down: float32 [2, 2304, 896], P(None, 'dp')
Outputs:
- output 1: bfloat16 [8, 896, 2304], P('rep'), parts along dimension 0
- output 2: bfloat16 [8, 896, 2304], P('rep'), parts along dimension 0
- output 3: bfloat16 [8, 2304, 896], P('rep'), parts along dimension 0
- output 4: float32 [8, 896, 2304], P('rep', 'dp'), parts along dimension 0
- output 5: float32 [8, 896, 2304], P('rep', 'dp'), parts along dimension 0
- output 6: float32 [8, 2304, 896], P('rep', 'dp'), parts along dimension 0
- output 7: float32 [8, 896, 2304], P('rep', 'dp'), parts along dimension 0
- output 8: float32 [8, 896, 2304], P('rep', 'dp'), parts along dimension 0
- output 9: float32 [8, 2304, 896], P('rep', 'dp'), parts along dimension 0
There are 4 independent parts. A program takes and returns all parts, laid end to end along the dimension named above; an argument that names none is the same for every part.
All inputs are finite; a program needn't handle non-finite values.
Results may differ from a plain program's by a relative error of at most 0.022.
Values are sent between devices in bfloat16 or wider.
A program may use at most 768 MiB of HBM per device.

v0:
```python
import jax
import jax.numpy as jnp
from jax import lax
from jax.sharding import PartitionSpec as P


def adamw(w, m, v, g):
    m = 0.9 * m + 0.1 * g
    v = 0.95 * v + 0.05 * g * g
    step = m * lax.rsqrt(v + 1e-8) + 0.1 * w
    return (w - 0.02 * step).astype(jnp.bfloat16), m, v


def solution(mesh):
    def step(*arrays):
        terms, weights, m, v = (arrays[i : i + 3] for i in (0, 3, 6, 9))
        gradients = [lax.psum_scatter(t[0], "dp", scatter_dimension=1, tiled=True).astype(jnp.float32) for t in terms]
        me = lax.axis_index("dp")
        own = [lax.dynamic_slice_in_dim(w, me * one.shape[1], one.shape[1], 1).astype(jnp.float32) for w, one in zip(weights, m, strict=True)]
        new = [adamw(w, m, v, g) for w, m, v, g in zip(own, m, v, gradients, strict=True)]
        whole = [lax.all_gather(one[0], "dp", axis=1, tiled=True) for one in new]
        return (*whole, *(one[1] for one in new), *(one[2] for one in new))

    all_of, cut = P(None, None, None), P(None, "dp", None)
    return jax.shard_map(
        step,
        mesh=mesh,
        in_specs=(P(("rep", "dp"), None, None, None),) * 3 + (all_of,) * 3 + (cut,) * 6,
        out_specs=(P("rep", None, None),) * 3 + (P("rep", "dp", None),) * 6,
        check_vma=False,
    )
```

profile of v0, /device:TPU:112, one launch (start us, length us, event | category | flops | bytes accessed | tf_op | source)
XLA Modules:
  0.0 514.3 jit_solution(17956225694219220129)
XLA Ops:
  7.2 0.1 reduce-scatter.8.cloned.1.call-start
  7.3 0.7 reduce-scatter.8.cloned.1.call-update
  8.0 0.1 reduce-scatter.6.cloned.1.call-start
  8.1 0.7 reduce-scatter.6.cloned.1.call-update
  8.8 0.1 reduce-scatter.4.cloned.1.call-start
  8.9 0.7 reduce-scatter.4.cloned.1.call-update
  9.6 0.1 all-gather.8.cloned.1.call-start
  9.7 79.0 %reduce-scatter.8.cloned.1.call-done = bf16[2,576,896]{2,1,0:T(8,128)(2,1)} async-done(((bf16[2,2304,896]{2,1,0:T(8,128)(2,1)}), bf16[2,576,896]{2,1,0:T(8,128)(2,1)}) %reduce-scatter.8.cloned.1.call-update) | async-done | bytes 2064400 | tf_op jit(solution)/shard_map/reduce_scatter | solution.py:17
  88.7 8.4 %fusion.10 = (bf16[2,576,896]{2,1,0:T(8,128)(2,1)}, f32[2,576,896]{2,1,0:T(8,128)}, f32[2,576,896]{2,1,0:T(8,128)}) fusion(bf16[2,2304,896]{2,1,0:T(8,128)(2,1)} %param.17, s32[]{:T(128)S(6)} %select_n.8, bf16[2,576,896]{2,1,0:T(8,128)(2,1)} %reduce-scatter.8.cloned.1.call-done, f32[2,576,896]{2,1,0:T(8,128)} %param.23, f32[2,576,896]{2,1,0:T(8,128)} %param.20), kind=kLoop, calls=%fused_computation.22 | loop fusion | flops 16515072 | bytes 22708228 | tf_op jit(solution)/shard_map/convert_element_type | solution.py:11
  97.1 0.1 all-gather.8.cloned.1.call-update
  97.1 0.1 all-gather.6.cloned.1.call-start
  97.2 69.0 %reduce-scatter.6.cloned.1.call-done = bf16[2,224,2304]{2,1,0:T(8,128)(2,1)} async-done(((bf16[2,896,2304]{2,1,0:T(8,128)(2,1)}), bf16[2,224,2304]{2,1,0:T(8,128)(2,1)}) %reduce-scatter.6.cloned.1.call-update) | async-done | bytes 2064400 | tf_op jit(solution)/shard_map/reduce_scatter | solution.py:17
  166.2 8.3 %fusion.6 = (bf16[2,224,2304]{2,1,0:T(8,128)(2,1)}, f32[2,224,2304]{2,1,0:T(8,128)}, f32[2,224,2304]{2,1,0:T(8,128)}) fusion(bf16[2,896,2304]{2,1,0:T(8,128)(2,1)} %param.16, s32[]{:T(128)S(6)} %select_n.7, bf16[2,224,2304]{2,1,0:T(8,128)(2,1)} %reduce-scatter.6.cloned.1.call-done, f32[2,224,2304]{2,1,0:T(8,128)} %param.22, f32[2,224,2304]{2,1,0:T(8,128)} %param.19), kind=kLoop, calls=%fused_computation.18 | loop fusion | flops 16515072 | bytes 22708228 | tf_op jit(solution)/shard_map/convert_element_type | solution.py:11
  174.5 0.1 all-gather.6.cloned.1.call-update
  174.6 0.1 all-gather.4.cloned.1.call-start
  174.6 69.0 %reduce-scatter.4.cloned.1.call-done = bf16[2,224,2304]{2,1,0:T(8,128)(2,1)} async-done(((bf16[2,896,2304]{2,1,0:T(8,128)(2,1)}), bf16[2,224,2304]{2,1,0:T(8,128)(2,1)}) %reduce-scatter.4.cloned.1.call-update) | async-done | bytes 2064400 | tf_op jit(solution)/shard_map/reduce_scatter | solution.py:17
  243.7 8.3 %fusion.2 = (bf16[2,224,2304]{2,1,0:T(8,128)(2,1)}, f32[2,224,2304]{2,1,0:T(8,128)}, f32[2,224,2304]{2,1,0:T(8,128)}) fusion(bf16[2,896,2304]{2,1,0:T(8,128)(2,1)} %param.15, s32[]{:T(128)S(6)} %select_n.7, bf16[2,224,2304]{2,1,0:T(8,128)(2,1)} %reduce-scatter.4.cloned.1.call-done, f32[2,224,2304]{2,1,0:T(8,128)} %param.21, f32[2,224,2304]{2,1,0:T(8,128)} %param.18), kind=kLoop, calls=%fused_computation.14 | loop fusion | flops 16515072 | bytes 22708228 | tf_op jit(solution)/shard_map/convert_element_type | solution.py:11
  252.0 0.1 all-gather.4.cloned.1.call-update
  252.1 71.4 %all-gather.8.cloned.1.call-done = bf16[2,2304,896]{2,1,0:T(8,128)(2,1)} async-done(((bf16[2,576,896]{2,1,0:T(8,128)(2,1)}), bf16[2,2304,896]{2,1,0:T(8,128)(2,1)}) %all-gather.8.cloned.1.call-update) | async-done | bytes 8257552 | tf_op jit(solution)/shard_map/all_gather | solution.py:21
  323.5 81.0 %all-gather.6.cloned.1.call-done = bf16[2,896,2304]{2,1,0:T(8,128)(2,1)} async-done(((bf16[2,224,2304]{2,1,0:T(8,128)(2,1)}), bf16[2,896,2304]{2,1,0:T(8,128)(2,1)}) %all-gather.6.cloned.1.call-update) | async-done | bytes 8257552 | tf_op jit(solution)/shard_map/all_gather | solution.py:21
  404.6 81.0 %all-gather.4.cloned.1.call-done = bf16[2,896,2304]{2,1,0:T(8,128)(2,1)} async-done(((bf16[2,224,2304]{2,1,0:T(8,128)(2,1)}), bf16[2,896,2304]{2,1,0:T(8,128)(2,1)}) %all-gather.4.cloned.1.call-update) | async-done | bytes 8257552 | tf_op jit(solution)/shard_map/all_gather | solution.py:21
  485.6 7.2 %copy.24 = bf16[2,896,2304]{2,1,0:T(8,128)(2,1)} copy(bf16[2,896,2304]{2,1,0:T(8,128)(2,1)} %all-gather.4.cloned.1.call-done) | data formatting | bytes 16515072
  492.8 7.2 %copy.25 = bf16[2,896,2304]{2,1,0:T(8,128)(2,1)} copy(bf16[2,896,2304]{2,1,0:T(8,128)(2,1)} %all-gather.6.cloned.1.call-done) | data formatting | bytes 16515072
  500.0 7.3 %copy.26 = bf16[2,2304,896]{2,1,0:T(8,128)(2,1)} copy(bf16[2,2304,896]{2,1,0:T(8,128)(2,1)} %all-gather.8.cloned.1.call-done) | data formatting | bytes 16515072
Async XLA Ops:
  7.2 81.5 %reduce-scatter.8.cloned.1.call-start = ((), (), s32[]{:S(2)}) async-start(), calls=%async_computation.7 | async-start | bytes 10321920 | tf_op jit(solution)/shard_map/reduce_scatter | solution.py:17
  8.0 158.2 %reduce-scatter.6.cloned.1.call-start = ((), (), s32[]{:S(2)}) async-start(), calls=%async_computation.5 | async-start | bytes 10321920 | tf_op jit(solution)/shard_map/reduce_scatter | solution.py:17
  8.8 234.9 %reduce-scatter.4.cloned.1.call-start = ((), (), s32[]{:S(2)}) async-start(), calls=%async_computation.3 | async-start | bytes 10321920 | tf_op jit(solution)/shard_map/reduce_scatter | solution.py:17
  9.6 313.9 %all-gather.8.cloned.1.call-start = ((), (), s32[]{:S(2)}) async-start(), calls=%async_computation.8 | async-start | bytes 10321920 | tf_op jit(solution)/shard_map/all_gather | solution.py:21
  97.1 307.4 %all-gather.6.cloned.1.call-start = ((), (), s32[]{:S(2)}) async-start(), calls=%async_computation.6 | async-start | bytes 10321920 | tf_op jit(solution)/shard_map/all_gather | solution.py:21
  174.6 311.0 %all-gather.4.cloned.1.call-start = ((), (), s32[]{:S(2)}) async-start(), calls=%async_computation.4 | async-start | bytes 10321920 | tf_op jit(solution)/shard_map/all_gather | solution.py:21
Sparse Core Ops, SparseCore 0:
  10.4 78.2 reduce-scatter.7
  91.1 75.0 reduce-scatter.5
  168.6 75.0 reduce-scatter.3
  245.7 77.8 all-gather.7
  325.5 79.0 all-gather.5
  406.5 79.0 all-gather.3
where the time goes:
time: 514 us
  waiting for transfers between devices  453 us (88%)
  other arithmetic  25 us (5%)
  local copies, waits for them, and re-layouts  21.8 us (4%)
  between operations  14.2 us (3%)
    all_gather x3, waiting for transfers between devices, step(): whole = [lax.all_gather(one[0], 'dp', axis=1, tiled=True) for one in new]  234 us
    reduce_scatter x3, waiting for transfers between devices, step(): lax.psum_scatter(t[0], 'dp', scatter_dimension=1, tiled=True)  217 us
    convert_element_type x3, other arithmetic, adamw(): return ((w - 0.02 * step).astype(jnp.bfloat16), m, v)  25 us
    unnamed x3, local copies, waits for them, and re-layouts  21.8 us
  transfers between devices with their start and end apart: 6, of which 6 were waited for; matrix products, arithmetic and copies ran while one was open for 5% of the time, Pallas kernels for 0%

commit v1 on v0

v1 whole, which is shorter than its diff:
```python
import jax
import jax.numpy as jnp
from jax import lax
from jax.experimental import pallas as pl
from jax.experimental.pallas import tpu as pltpu
from jax.sharding import PartitionSpec as P

MESH = pl.DeviceIdType.MESH
TILE = 16
RIGHT, LEFT = 0, 1


def adamw(w, m, v, g):
    m = 0.9 * m + 0.1 * g
    v = 0.95 * v + 0.05 * g * g
    step = m * lax.rsqrt(v + 1e-8) + 0.1 * w
    return (w - 0.02 * step).astype(jnp.bfloat16), m, v


def kernel(n, *refs):
    terms, weights, ms, vs, w_outs, m_outs, v_outs, partials, raws, sums, staged = (refs[i : i + 3] for i in range(0, 33, 3))
    (bufs, one_send, one_recv, two_send, two_recv, local, early) = refs[33:]
    me = lax.axis_index("dp")
    right, left, across = lax.rem(me + 1, n), lax.rem(me + n - 1, n), lax.rem(me + 2, n)
    neighbours = (right, left)

    def rows(t, owner, half):
        depth = w_outs[t].shape[1] // n // 2
        return pl.ds(pl.multiple_of((owner * 2 + half) * depth, 16), depth)

    barrier = pltpu.get_barrier_semaphore()
    for neighbour in neighbours:
        pl.semaphore_signal(barrier, 1, device_id={"dp": neighbour}, device_id_type=MESH)
    pl.semaphore_wait(barrier, 2)

    matrices = [(t, layer) for t in range(3) for layer in range(2)]

    def remote(kind, t, layer, way, src, dst):
        at = (kind, 2 * t + layer, way)
        return pltpu.make_async_remote_copy(
            src, dst, one_send.at[at], one_recv.at[at], device_id={"dp": neighbours[way]}, device_id_type=MESH
        )

    def far(t, layer, way):
        return remote(0, t, layer, way, terms[t].at[0, layer, rows(t, across, way)], partials[t].at[way, layer])

    def near(t, layer, way):
        return remote(1, t, layer, way, terms[t].at[0, layer, rows(t, neighbours[way], 1 - way)], raws[t].at[way, layer])

    def added(t, layer, way):
        return remote(2, t, layer, way, staged[t].at[way, layer], sums[t].at[way, layer])

    def onward(t, layer, way):
        half = w_outs[t].at[layer, rows(t, neighbours[1 - way], way)]
        return remote(3, t, layer, way, half, half)

    def direct(t, layer, way, half):
        at = (2 * t + layer, way, half)
        block = w_outs[t].at[layer, rows(t, me, half)]
        return pltpu.make_async_remote_copy(
            block, block, two_send.at[at], two_recv.at[at], device_id={"dp": neighbours[way]}, device_id_type=MESH
        )

    for t, layer in matrices:
        for send in (far, near):
            for way in (RIGHT, LEFT):
                send(t, layer, way).start()

    def own(t):
        copies = [pltpu.make_async_copy(ms[t], m_outs[t], early.at[t, 0]), pltpu.make_async_copy(vs[t], v_outs[t], early.at[t, 1])]
        for layer in range(2):
            depth = w_outs[t].shape[1] // n
            block = pl.ds(pl.multiple_of(me * depth, 16), depth)
            copies.append(pltpu.make_async_copy(weights[t].at[layer, block], w_outs[t].at[layer, block], early.at[t, 2 + layer]))
        return copies

    for t in range(3):
        for copy in own(t):
            copy.start()

    def views(t):
        depth, width = staged[t].shape[2:]
        return [bufs[1 if t == 2 else 0].at[i] for i in range(4)], depth, width

    def fetch(copies):
        for copy in copies:
            copy.start()
        for copy in copies:
            copy.wait()

    for t, layer in matrices:
        (mine, other, _, out), depth, width = views(t)
        for way in (RIGHT, LEFT):
            far(t, layer, way).wait_recv()
            fetch(
                [
                    pltpu.make_async_copy(terms[t].at[0, layer, rows(t, neighbours[way], way)], mine, local.at[0]),
                    pltpu.make_async_copy(partials[t].at[way, layer], other, local.at[1]),
                ]
            )

            def add(i, _):
                at = pl.ds(pl.multiple_of(i * TILE, TILE), TILE)
                out[at] = (mine[at].astype(jnp.float32) + other[at].astype(jnp.float32)).astype(jnp.bfloat16)
                return 0

            lax.fori_loop(0, depth // TILE, add, 0)
            fetch([pltpu.make_async_copy(out, staged[t].at[way, layer], local.at[2])])
            added(t, layer, way).start()

    for t, layer in matrices:
        (mine, one, two, _), depth, width = views(t)
        if layer == 0:
            for copy in own(t):
                copy.wait()
        for half in (0, 1):
            added(t, layer, half).wait_recv()
            near(t, layer, 1 - half).wait_recv()
            fetch(
                [
                    pltpu.make_async_copy(terms[t].at[0, layer, rows(t, me, half)], mine, local.at[0]),
                    pltpu.make_async_copy(sums[t].at[half, layer], one, local.at[1]),
                    pltpu.make_async_copy(raws[t].at[1 - half, layer], two, local.at[2]),
                ]
            )

            def update(i, _):
                at = pl.ds(pl.multiple_of(i * TILE, TILE), TILE)
                block = pl.ds(pl.multiple_of(half * depth + i * TILE, TILE), TILE)
                place = pl.ds(pl.multiple_of((me * 2 + half) * depth + i * TILE, TILE), TILE)
                g = mine[at].astype(jnp.float32) + one[at].astype(jnp.float32) + two[at].astype(jnp.float32)
                g = g.astype(jnp.bfloat16).astype(jnp.float32)
                w = w_outs[t][layer, place].astype(jnp.float32)
                w, m, v = adamw(w, m_outs[t][layer, block], v_outs[t][layer, block], g)
                w_outs[t][layer, place] = w
                m_outs[t][layer, block] = m
                v_outs[t][layer, block] = v
                return 0

            lax.fori_loop(0, depth // TILE, update, 0)
            for way in (RIGHT, LEFT):
                direct(t, layer, way, half).start()

    for t, layer in matrices:
        for way in (RIGHT, LEFT):
            direct(t, layer, way, way).wait_recv()
            onward(t, layer, way).start()

    for t, layer in matrices:
        for way in (RIGHT, LEFT):
            for send in (far, near, added):
                send(t, layer, way).wait_send()
            direct(t, layer, way, 1 - way).wait_recv()
            for half in (0, 1):
                direct(t, layer, way, half).wait_send()
    for t, layer in matrices:
        for way in (RIGHT, LEFT):
            onward(t, layer, way).wait()


def unload(*refs):
    half = len(refs) // 2
    copies = [pltpu.make_async_copy(src, dst, refs[-1].at[i]) for i, (src, dst) in enumerate(zip(refs[:half], refs[half:-1], strict=True))]
    for copy in copies:
        copy.start()
    for copy in copies:
        copy.wait()


def to_hbm(arrays):
    return pl.pallas_call(
        unload,
        out_shape=[jax.ShapeDtypeStruct(a.shape, a.dtype) for a in arrays],
        in_specs=[pl.BlockSpec(memory_space=pltpu.VMEM)] * len(arrays),
        out_specs=[pl.BlockSpec(memory_space=pltpu.HBM)] * len(arrays),
        scratch_shapes=[pltpu.SemaphoreType.DMA((len(arrays),))],
        compiler_params=pltpu.CompilerParams(vmem_limit_bytes=2**20),
        name="unload",
    )(*arrays)


def solution(mesh):
    n = mesh.shape["dp"]

    def step(*arrays):
        terms, weights, ms, vs = (arrays[i : i + 3] for i in (0, 3, 6, 9))
        hbm = pl.BlockSpec(memory_space=pltpu.HBM)
        vmem = pl.BlockSpec(memory_space=pltpu.VMEM)
        halves = [(w.shape[0], w.shape[1] // n // 2, w.shape[2]) for w in weights]
        slots = [pltpu.HBM((2, *half), jnp.bfloat16) for half in halves] * 4
        out = pl.pallas_call(
            lambda *refs: kernel(n, *refs),
            out_shape=(
                *(pltpu.VMEM(w.shape, w.dtype) for w in weights),
                *(pltpu.VMEM(m.shape, m.dtype) for m in ms),
                *(pltpu.VMEM(v.shape, v.dtype) for v in vs),
                *slots,
            ),
            in_specs=[hbm] * 12,
            out_specs=(*([vmem] * 9), *([hbm] * 12)),
            scratch_shapes=[
                [pltpu.VMEM((4, *halves[0][1:]), jnp.bfloat16), pltpu.VMEM((4, *halves[2][1:]), jnp.bfloat16)],
                pltpu.SemaphoreType.DMA((4, 6, 2)),
                pltpu.SemaphoreType.DMA((4, 6, 2)),
                pltpu.SemaphoreType.DMA((6, 2, 2)),
                pltpu.SemaphoreType.DMA((6, 2, 2)),
                pltpu.SemaphoreType.DMA((3,)),
                pltpu.SemaphoreType.DMA((3, 4)),
            ],
            compiler_params=pltpu.CompilerParams(collective_id=0, has_side_effects=True, vmem_limit_bytes=8 * 2**20),
            name="sharded_adamw",
        )(*terms, *weights, *ms, *vs)
        return to_hbm(out[:9])

    all_of, cut = P(None, None, None), P(None, "dp", None)
    return jax.shard_map(
        step,
        mesh=mesh,
        in_specs=(P(("rep", "dp"), None, None, None),) * 3 + (all_of,) * 3 + (cut,) * 6,
        out_specs=(P("rep", None, None),) * 3 + (P("rep", "dp", None),) * 6,
        check_vma=False,
    )
```

time: 514 us -> 422 us (0.82)
  waiting for transfers between devices: 453 us -> 0 us
  Pallas kernels: 0 us -> 421 us
  other arithmetic: 25 us -> 0 us
  local copies, waits for them, and re-layouts: 21.8 us -> 0 us
  between operations: 14.2 us -> 0.65 us
    pallas_call x0 -> x2, Pallas kernels: none -> 421 us  [the longest x1 405 us: step(): pl.pallas_call(lambda *refs: kernel(n, *refs), out_shape=(*(pltpu.VMEM(w....]
    all_gather x3 -> x0, waiting for transfers between devices: 234 us -> none  [step(): whole = [lax.all_gather(one[0], 'dp', axis=1, tiled=True) for one in new]]
    reduce_scatter x3 -> x0, waiting for transfers between devices: 217 us -> none  [step(): lax.psum_scatter(t[0], 'dp', scatter_dimension=1, tiled=True)]
    convert_element_type x3 -> x0, other arithmetic: 25 us -> none  [adamw(): return ((w - 0.02 * step).astype(jnp.bfloat16), m, v)]
    unnamed x3 -> x0, local copies, waits for them, and re-layouts: 21.8 us -> none
  transfers between devices with their start and end apart: 6 -> 0, of which waited for: 6 -> 0; matrix products, arithmetic and copies ran while one was open for 5% -> 0% of each run, Pallas kernels for 0% -> 0%
where the time goes in v1:
time: 422 us; the launch traced here: 421 us
  Pallas kernels  421 us (100%)
    pallas_call x1, Pallas kernels, step(): pl.pallas_call(lambda *refs: kernel(n, *refs), out_shape=(*(pltpu.VMEM(w....  405 us
    pallas_call x1, Pallas kernels, to_hbm(): pl.pallas_call(unload, out_shape=[jax.ShapeDtypeStruct(a.shape, a.dtype)...  16 us

profile of v1, /device:TPU:112, one launch (start us, length us, event | category | flops | bytes accessed | tf_op | source)
XLA Modules:
  0.0 421.3 jit_solution(12641235535657102423)
XLA Ops:
  0.6 404.7 %sharded_adamw.1 = (bf16[2,896,2304]{2,1,0:T(8,128)(2,1)S(1)}, bf16[2,896,2304]{2,1,0:T(8,128)(2,1)S(1)}, bf16[2,2304,896]{2,1,0:T(8,128)(2,1)S(1)}, f32[2,224,2...) custom-call(bf16[1,2,896,2304]{3,2,1,0:T(8,128)(2,1)} %refs_0_.1, ...), custom_call_target="tpu_custom_call" | custom-call | tf_op jit(solution)/shard_map/sharded_adamw/pallas_call | solution.py:191
  405.4 16.0 %unload.1 = (bf16[2,896,2304]{2,1,0:T(8,128)(2,1)}, bf16[2,896,2304]{2,1,0:T(8,128)(2,1)}, bf16[2,2304,896]{2,1,0:T(8,128)(2,1)}, f32[2,224,2304]{2,1,0:T(8,128)...) custom-call(bf16[2,896,2304]{2,1,0:T(8,128)(2,1)S(1)} %get-tuple-ele, ...), custom_call_target="tpu_custom_call" | custom-call | tf_op jit(solution)/shard_map/unload/pallas_call | solution.py:171

commit v2 on v1

--- a/solution.py
+++ b/solution.py
@@ -19,7 +19,7 @@
 
 def kernel(n, *refs):
     terms, weights, ms, vs, w_outs, m_outs, v_outs, partials, raws, sums, staged = (refs[i : i + 3] for i in range(0, 33, 3))
-    (bufs, one_send, one_recv, two_send, two_recv, local, early) = refs[33:]
+    passed, (bufs, one_send, one_recv, two_send, two_recv, local, early) = refs[33:35], refs[35:]
     me = lax.axis_index("dp")
     right, left, across = lax.rem(me + 1, n), lax.rem(me + n - 1, n), lax.rem(me + 2, n)
     neighbours = (right, left)
@@ -57,8 +57,9 @@
     def direct(t, layer, way, half):
         at = (2 * t + layer, way, half)
         block = w_outs[t].at[layer, rows(t, me, half)]
+        there = passed[way].at[layer] if t == 2 and way == half else block
         return pltpu.make_async_remote_copy(
-            block, block, two_send.at[at], two_recv.at[at], device_id={"dp": neighbours[way]}, device_id_type=MESH
+            block, there, two_send.at[at], two_recv.at[at], device_id={"dp": neighbours[way]}, device_id_type=MESH
         )
 
     for t, layer in matrices:
@@ -144,7 +145,8 @@
     for t, layer in matrices:
         for way in (RIGHT, LEFT):
             direct(t, layer, way, way).wait_recv()
-            onward(t, layer, way).start()
+            if t < 2:
+                onward(t, layer, way).start()
 
     for t, layer in matrices:
         for way in (RIGHT, LEFT):
@@ -153,30 +155,71 @@
             direct(t, layer, way, 1 - way).wait_recv()
             for half in (0, 1):
                 direct(t, layer, way, half).wait_send()
-    for t, layer in matrices:
+    for t, layer in matrices[:4]:
         for way in (RIGHT, LEFT):
             onward(t, layer, way).wait()
 
 
-def unload(*refs):
-    half = len(refs) // 2
-    copies = [pltpu.make_async_copy(src, dst, refs[-1].at[i]) for i, (src, dst) in enumerate(zip(refs[:half], refs[half:-1], strict=True))]
+def unload_kernel(n, *refs):
+    passed, arrays, outs, (sem, block_sem) = refs[:2], refs[2:11], refs[11:20], refs[20:]
+    me = lax.axis_index("dp")
+    right, left = lax.rem(me + 1, n), lax.rem(me + n - 1, n)
+    depth = passed[0].shape[1]
+    copies = [pltpu.make_async_copy(arrays[i], outs[i], sem.at[i]) for i in range(9) if i != 2]
+
+    def rows(owner, half, halves=1):
+        return pl.ds(pl.multiple_of((owner * 2 + half) * depth, 16), halves * depth)
+
+    for layer in range(2):
+        here = [arrays[2].at[layer, at] for at in (rows(me, 0, 2), rows(right, 0), rows(left, 1))]
+        here += [passed[way].at[layer] for way in (RIGHT, LEFT)]
+        there = [rows(me, 0, 2), rows(right, 0), rows(left, 1), rows(left, RIGHT), rows(right, LEFT)]
+        copies += [pltpu.make_async_copy(a, outs[2].at[layer, at], block_sem.at[layer, i]) for i, (a, at) in enumerate(zip(here, there, strict=True))]
     for copy in copies:
         copy.start()
     for copy in copies:
         copy.wait()
 
 
-def to_hbm(arrays):
+def unload(n, passed, arrays):
+    hbm, vmem = pl.BlockSpec(memory_space=pltpu.HBM), pl.BlockSpec(memory_space=pltpu.VMEM)
+    moved = sum(a.size * a.dtype.itemsize for a in arrays)
     return pl.pallas_call(
-        unload,
+        lambda *refs: unload_kernel(n, *refs),
         out_shape=[jax.ShapeDtypeStruct(a.shape, a.dtype) for a in arrays],
-        in_specs=[pl.BlockSpec(memory_space=pltpu.VMEM)] * len(arrays),
-        out_specs=[pl.BlockSpec(memory_space=pltpu.HBM)] * len(arrays),
-        scratch_shapes=[pltpu.SemaphoreType.DMA((len(arrays),))],
+        in_specs=[vmem] * (2 + len(arrays)),
+        out_specs=[hbm] * len(arrays),
+        scratch_shapes=[pltpu.SemaphoreType.DMA((len(arrays),)), pltpu.SemaphoreType.DMA((2, 5))],
         compiler_params=pltpu.CompilerParams(vmem_limit_bytes=2**20),
+        cost_estimate=pl.CostEstimate(flops=moved * 64, bytes_accessed=moved, transcendentals=0),
         name="unload",
-    )(*arrays)
+    )(*passed, *arrays)
+
+
+def finish_kernel(n, a, b, w, out, sem):
+    depth = a.shape[1]
+    owner = lax.rem(lax.axis_index("dp") + 2, n)
+    copies = []
+    for half, x in enumerate((a, b)):
+        rows = pl.ds(pl.multiple_of((owner * 2 + half) * depth, 16), depth)
+        copies.append(pltpu.make_async_copy(x, out.at[:, rows], sem.at[half]))
+        copies[-1].start()
+    for copy in copies:
+        copy.wait()
+
+
+def finish(n, halves, w):
+    hbm, vmem = pl.BlockSpec(memory_space=pltpu.HBM), pl.BlockSpec(memory_space=pltpu.VMEM)
+    return pl.pallas_call(
+        lambda *refs: finish_kernel(n, *refs),
+        out_shape=jax.ShapeDtypeStruct(w.shape, w.dtype),
+        in_specs=[vmem, vmem, hbm],
+        out_specs=hbm,
+        scratch_shapes=[pltpu.SemaphoreType.DMA((2,))],
+        input_output_aliases={2: 0},
+        compiler_params=pltpu.CompilerParams(vmem_limit_bytes=2**20),
+        name="finish",
+    )(*halves, w)
 
 
 def solution(mesh):
@@ -195,9 +238,10 @@
                 *(pltpu.VMEM(m.shape, m.dtype) for m in ms),
                 *(pltpu.VMEM(v.shape, v.dtype) for v in vs),
                 *slots,
+                *([pltpu.HBM(halves[2], jnp.bfloat16)] * 2),
             ),
             in_specs=[hbm] * 12,
-            out_specs=(*([vmem] * 9), *([hbm] * 12)),
+            out_specs=(*([vmem] * 9), *([hbm] * 14)),
             scratch_shapes=[
                 [pltpu.VMEM((4, *halves[0][1:]), jnp.bfloat16), pltpu.VMEM((4, *halves[2][1:]), jnp.bfloat16)],
                 pltpu.SemaphoreType.DMA((4, 6, 2)),
@@ -210,7 +254,11 @@
             compiler_params=pltpu.CompilerParams(collective_id=0, has_side_effects=True, vmem_limit_bytes=8 * 2**20),
             name="sharded_adamw",
         )(*terms, *weights, *ms, *vs)
-        return to_hbm(out[:9])
+        passed = out[21:]
+        ring = [[(i, (i + by) % n) for i in range(n)] for by in (1, n - 1)]
+        halves_across = [lax.ppermute(x, "dp", to) for x, to in zip(passed, ring, strict=True)]
+        done = unload(n, passed, out[:9])
+        return (*done[:2], finish(n, halves_across, done[2]), *done[3:])
 
     all_of, cut = P(None, None, None), P(None, "dp", None)
     return jax.shard_map(

time: 422 us -> 410 us (0.972)
  Pallas kernels: 421 us -> 399 us
    pallas_call x1, Pallas kernels: 405 us -> 383 us  [step(): pl.pallas_call(lambda *refs: kernel(n, *refs), out_shape=(*(pltpu.VMEM(w....]
    pallas_call x1 -> x2, Pallas kernels: 16 us -> 16.6 us  [the longest x1 15.3 us: unload(): pl.pallas_call(lambda *refs: unload_kernel(n, *refs), out_shape=[jax.Shap...]
  transfers between devices with their start and end apart: 0 -> 2, of which waited for: 0 -> 1; matrix products, arithmetic and copies ran while one was open for 0% -> 0% of each run, Pallas kernels for 0% -> 4%
where the time goes in v2:
time: 410 us
  Pallas kernels  399 us (97%)
    pallas_call x1, Pallas kernels, step(): pl.pallas_call(lambda *refs: kernel(n, *refs), out_shape=(*(pltpu.VMEM(w....  383 us
    pallas_call x1, Pallas kernels, unload(): pl.pallas_call(lambda *refs: unload_kernel(n, *refs), out_shape=[jax.Shap...  15.3 us
  transfers between devices with their start and end apart: 2, of which 1 were waited for; matrix products, arithmetic and copies ran while one was open for 0% of the time, Pallas kernels for 4%

profile of v2, /device:TPU:112, one launch (start us, length us, event | category | flops | bytes accessed | tf_op | source)
XLA Modules:
  0.0 409.6 jit_solution(14921888841058874601)
XLA Ops:
  0.6 382.6 %sharded_adamw.1 = (bf16[2,896,2304]{2,1,0:T(8,128)(2,1)S(1)}, bf16[2,896,2304]{2,1,0:T(8,128)(2,1)S(1)}, bf16[2,2304,896]{2,1,0:T(8,128)(2,1)S(1)}, f32[2,224,2...) custom-call(bf16[1,2,896,2304]{3,2,1,0:T(8,128)(2,1)} %refs_0_.1, ...), custom_call_target="tpu_custom_call" | custom-call | tf_op jit(solution)/shard_map/sharded_adamw/pallas_call | solution.py:234
  383.3 1.4 collective-permute-start
  384.7 1.9 collective-permute-start.1
  386.6 0.0 copy-start
  386.6 1.2 copy-done
  387.8 0.0 copy-start.1
  387.8 1.2 copy-done.1
  389.0 15.3 %unload.1 = (bf16[2,896,2304]{2,1,0:T(8,128)(2,1)}, bf16[2,896,2304]{2,1,0:T(8,128)(2,1)}, bf16[2,2304,896]{2,1,0:T(8,128)(2,1)}, f32[2,224,2304]{2,1,0:T(8,128)...) custom-call(bf16[2,288,896]{2,1,0:T(8,128)(2,1)S(1)} %copy-done.1, ...), custom_call_target="tpu_custom_call" | custom-call | flops 3170893824 | bytes 49545216 | tf_op jit(solution)/shard_map/unload/pallas_call | solution.py:187
  404.3 4.0 collective-permute-done.refs_0_
  408.3 0.0 collective-permute-done.1.refs_1_
  408.3 1.3 finish.1
Async XLA Ops:
  383.3 25.1 %collective-permute-start = (bf16[2,288,896]{2,1,0:T(8,128)(2,1)}, bf16[2,288,896]{2,1,0:T(8,128)(2,1)S(1)}, u32[]{:S(2)}, u32[]{:S(2)}) collective-permute-start(bf16[2,288,896]{2,1,0:T(8,128)(2,1)} %get-tuple-element.29.refs_0_), channel_id=1, source_target_pairs={{0,1},{1,2},{2,3},{3,0},{4,5},{5,6},{6,7},{7,4},{8,9},{9,10},{10,1... | collective-permute-start | bytes 3096584 | tf_op jit(solution)/shard_map/ppermute | solution.py:259
  384.7 23.6 %collective-permute-start.1 = (bf16[2,288,896]{2,1,0:T(8,128)(2,1)}, bf16[2,288,896]{2,1,0:T(8,128)(2,1)S(1)}, u32[]{:S(2)}, u32[]{:S(2)}) collective-permute-start(bf16[2,288,896]{2,1,0:T(8,128)(2,1)} %get-tuple-element.30.refs_1_), channel_id=1, source_target_pairs={{0,3},{1,0},{2,1},{3,2},{4,7},{5,4},{6,5},{7,6},{8,11},{9,8},{10,9... | collective-permute-start | bytes 3096584 | tf_op jit(solution)/shard_map/ppermute | solution.py:259
  386.6 1.2 copy-start
  387.8 1.2 copy-start.1

commit v3 on v0

v3 whole, which is shorter than its diff:
```python
import jax
import jax.numpy as jnp
from jax import lax
from jax.experimental import pallas as pl
from jax.experimental.pallas import tpu as pltpu
from jax.sharding import PartitionSpec as P

MESH = pl.DeviceIdType.MESH
TILE = 16
RIGHT, LEFT = 0, 1
LAST = 2


def adamw(w, m, v, g):
    m = 0.9 * m + 0.1 * g
    v = 0.95 * v + 0.05 * g * g
    step = m * lax.rsqrt(v + 1e-8) + 0.1 * w
    return (w - 0.02 * step).astype(jnp.bfloat16), m, v


def ring(n):
    me = lax.axis_index("dp")
    return me, (lax.rem(me + 1, n), lax.rem(me + n - 1, n))


def at_row(start, size):
    return pl.ds(pl.multiple_of(start, 16), size)


def fetch(*copies):
    for copy in copies:
        copy.start()
    for copy in copies:
        copy.wait()


def kernel(n, *refs):
    terms, weights, ms, vs, w_outs, m_outs, v_outs, partials, raws, sums, staged = (refs[i : i + 3] for i in range(0, 33, 3))
    passed, (bufs, one_send, one_recv, two_send, two_recv, local, early) = refs[33:35], refs[35:]
    me, neighbours = ring(n)
    across = lax.rem(me + 2, n)
    halves = [w.shape[1] // n // 2 for w in w_outs]

    def rows(t, owner, half):
        return at_row((owner * 2 + half) * halves[t], halves[t])

    barrier = pltpu.get_barrier_semaphore()
    for neighbour in neighbours:
        pl.semaphore_signal(barrier, 1, device_id={"dp": neighbour}, device_id_type=MESH)
    pl.semaphore_wait(barrier, 2)

    def remote(way, src, dst, send, recv):
        return pltpu.make_async_remote_copy(src, dst, send, recv, device_id={"dp": neighbours[way]}, device_id_type=MESH)

    def one(kind, t, way, src, dst):
        return remote(way, src, dst, one_send.at[kind, t, way], one_recv.at[kind, t, way])

    def far(t, way):
        return one(0, t, way, terms[t].at[0, :, rows(t, across, way)], partials[t].at[way])

    def near(t, way):
        return one(1, t, way, terms[t].at[0, :, rows(t, neighbours[way], 1 - way)], raws[t].at[way])

    def added(t, way):
        return one(2, t, way, staged[t].at[way], sums[t].at[way])

    def onward(t, way):
        half = w_outs[t].at[:, rows(t, neighbours[1 - way], way)]
        return one(3, t, way, half, half)

    def direct(t, way):
        if t != LAST:
            block = w_outs[t].at[:, at_row(me * 2 * halves[t], 2 * halves[t])]
            return [remote(way, block, block, two_send.at[t, way, 0], two_recv.at[t, way, 0])]
        copies = []
        for part in (0, 1):
            block = w_outs[t].at[:, rows(t, me, part)]
            there = passed[way] if part == way else block
            copies.append(remote(way, block, there, two_send.at[t, way, part], two_recv.at[t, way, part]))
        return copies

    for t in range(3):
        for send in (far, near):
            for way in (RIGHT, LEFT):
                send(t, way).start()

    def own(t):
        block = at_row(me * 2 * halves[t], 2 * halves[t])
        return [
            pltpu.make_async_copy(ms[t], m_outs[t], early.at[t, 0]),
            pltpu.make_async_copy(vs[t], v_outs[t], early.at[t, 1]),
            pltpu.make_async_copy(weights[t].at[:, block], w_outs[t].at[:, block], early.at[t, 2]),
        ]

    for t in range(3):
        for copy in own(t):
            copy.start()

    def each_tile(t, body):
        steps = halves[t] // TILE

        def step(i, _):
            body(i // steps, lax.rem(i, steps) * TILE)
            return 0

        lax.fori_loop(0, 2 * steps, step, 0)

    for t in range(3):
        mine, other, _ = (bufs[t == LAST].at[i] for i in range(3))
        for way in (RIGHT, LEFT):
            far(t, way).wait_recv()
            fetch(
                pltpu.make_async_copy(terms[t].at[0, :, rows(t, neighbours[way], way)], mine, local.at[0]),
                pltpu.make_async_copy(partials[t].at[way], other, local.at[1]),
            )

            def add(layer, row):
                at = (layer, at_row(row, TILE))
                mine[at] = (mine[at].astype(jnp.float32) + other[at].astype(jnp.float32)).astype(jnp.bfloat16)

            each_tile(t, add)
            fetch(pltpu.make_async_copy(mine, staged[t].at[way], local.at[2]))
            added(t, way).start()

    for t in range(3):
        mine, first, second = (bufs[t == LAST].at[i] for i in range(3))
        for copy in own(t):
            copy.wait()
        for half in (0, 1):
            added(t, half).wait_recv()
            near(t, 1 - half).wait_recv()
            fetch(
                pltpu.make_async_copy(terms[t].at[0, :, rows(t, me, half)], mine, local.at[0]),
                pltpu.make_async_copy(sums[t].at[half], first, local.at[1]),
                pltpu.make_async_copy(raws[t].at[1 - half], second, local.at[2]),
            )

            def update(layer, row):
                at = (layer, at_row(row, TILE))
                block = (layer, at_row(half * halves[t] + row, TILE))
                place = (layer, at_row((me * 2 + half) * halves[t] + row, TILE))
                g = mine[at].astype(jnp.float32) + first[at].astype(jnp.float32) + second[at].astype(jnp.float32)
                g = g.astype(jnp.bfloat16).astype(jnp.float32)
                w, m, v = adamw(w_outs[t][place].astype(jnp.float32), m_outs[t][block], v_outs[t][block], g)
                w_outs[t][place] = w
                m_outs[t][block] = m
                v_outs[t][block] = v

            each_tile(t, update)
        for way in (RIGHT, LEFT):
            for copy in direct(t, way):
                copy.start()

    for t in range(LAST):
        for way in (RIGHT, LEFT):
            direct(t, way)[0].wait_recv()
            onward(t, way).start()

    for t in range(3):
        for way in (RIGHT, LEFT):
            for send in (far, near, added):
                send(t, way).wait_send()
            for copy in direct(t, way):
                copy.wait_send()
                if t == LAST:
                    copy.wait_recv()
    for t in range(LAST):
        for way in (RIGHT, LEFT):
            onward(t, way).wait()


def unload_kernel(n, *refs):
    passed, arrays, outs, (sem, block_sem) = refs[:2], refs[2:11], refs[11:20], refs[20:]
    me, (right, left) = ring(n)
    w, w_out = arrays[LAST], outs[LAST]
    cut, rest = (x.shape[1] for x in passed)
    depth = cut + rest
    copies = [pltpu.make_async_copy(arrays[i], outs[i], sem.at[i]) for i in range(len(arrays)) if i != LAST]
    here = [at_row(me * depth, depth), at_row(right * depth, cut), at_row(left * depth + cut, rest)]
    copies += [pltpu.make_async_copy(w.at[:, at], w_out.at[:, at], block_sem.at[i]) for i, at in enumerate(here)]
    there = [at_row(left * depth, cut), at_row(right * depth + cut, rest)]
    copies += [pltpu.make_async_copy(passed[way], w_out.at[:, at], block_sem.at[3 + way]) for way, at in enumerate(there)]
    fetch(*copies)


def unload(n, passed, arrays):
    hbm, vmem = pl.BlockSpec(memory_space=pltpu.HBM), pl.BlockSpec(memory_space=pltpu.VMEM)
    moved = sum(a.size * a.dtype.itemsize for a in arrays)
    return pl.pallas_call(
        lambda *refs: unload_kernel(n, *refs),
        out_shape=[jax.ShapeDtypeStruct(a.shape, a.dtype) for a in arrays],
        in_specs=[vmem] * (2 + len(arrays)),
        out_specs=[hbm] * len(arrays),
        scratch_shapes=[pltpu.SemaphoreType.DMA((len(arrays),)), pltpu.SemaphoreType.DMA((5,))],
        compiler_params=pltpu.CompilerParams(vmem_limit_bytes=2**20),
        cost_estimate=pl.CostEstimate(flops=moved * 64, bytes_accessed=moved, transcendentals=0),
        name="unload",
    )(*passed, *arrays)


def finish_kernel(n, a, b, w, out, sem):
    cut, rest = a.shape[1], b.shape[1]
    start = lax.rem(lax.axis_index("dp") + 2, n) * (cut + rest)
    fetch(
        pltpu.make_async_copy(a, out.at[:, at_row(start, cut)], sem.at[0]),
        pltpu.make_async_copy(b, out.at[:, at_row(start + cut, rest)], sem.at[1]),
    )


def finish(n, parts, w):
    hbm, vmem = pl.BlockSpec(memory_space=pltpu.HBM), pl.BlockSpec(memory_space=pltpu.VMEM)
    return pl.pallas_call(
        lambda *refs: finish_kernel(n, *refs),
        out_shape=jax.ShapeDtypeStruct(w.shape, w.dtype),
        in_specs=[vmem, vmem, hbm],
        out_specs=hbm,
        scratch_shapes=[pltpu.SemaphoreType.DMA((2,))],
        input_output_aliases={2: 0},
        compiler_params=pltpu.CompilerParams(vmem_limit_bytes=2**20),
        name="finish",
    )(*parts, w)


def solution(mesh):
    n = mesh.shape["dp"]

    def step(*arrays):
        terms, weights, ms, vs = (arrays[i : i + 3] for i in (0, 3, 6, 9))
        hbm, vmem = pl.BlockSpec(memory_space=pltpu.HBM), pl.BlockSpec(memory_space=pltpu.VMEM)
        halves = [(w.shape[0], w.shape[1] // n // 2, w.shape[2]) for w in weights]
        slots = [pltpu.HBM((2, *half), jnp.bfloat16) for half in halves] * 4
        passed = [pltpu.HBM(halves[LAST], jnp.bfloat16)] * 2
        out = pl.pallas_call(
            lambda *refs: kernel(n, *refs),
            out_shape=(
                *(pltpu.VMEM(w.shape, w.dtype) for w in weights),
                *(pltpu.VMEM(m.shape, m.dtype) for m in ms),
                *(pltpu.VMEM(v.shape, v.dtype) for v in vs),
                *slots,
                *passed,
            ),
            in_specs=[hbm] * 12,
            out_specs=(*([vmem] * 9), *([hbm] * 14)),
            scratch_shapes=[
                [pltpu.VMEM((3, *halves[0]), jnp.bfloat16), pltpu.VMEM((3, *halves[LAST]), jnp.bfloat16)],
                pltpu.SemaphoreType.DMA((4, 3, 2)),
                pltpu.SemaphoreType.DMA((4, 3, 2)),
                pltpu.SemaphoreType.DMA((3, 2, 2)),
                pltpu.SemaphoreType.DMA((3, 2, 2)),
                pltpu.SemaphoreType.DMA((3,)),
                pltpu.SemaphoreType.DMA((3, 3)),
            ],
            compiler_params=pltpu.CompilerParams(collective_id=0, has_side_effects=True, vmem_limit_bytes=7 * 2**20),
            name="sharded_adamw",
        )(*terms, *weights, *ms, *vs)
        mine, passed = out[:9], out[21:]
        to = [[(i, (i + by) % n) for i in range(n)] for by in (1, n - 1)]
        parts = [lax.ppermute(x, "dp", way) for x, way in zip(passed, to, strict=True)]
        done = unload(n, passed, mine)
        return tuple(finish(n, parts, x) if i == LAST else x for i, x in enumerate(done))

    all_of, cut = P(None, None, None), P(None, "dp", None)
    return jax.shard_map(
        step,
        mesh=mesh,
        in_specs=(P(("rep", "dp"), None, None, None),) * 3 + (all_of,) * 3 + (cut,) * 6,
        out_specs=(P("rep", None, None),) * 3 + (P("rep", "dp", None),) * 6,
        check_vma=False,
    )
```

time: 514 us -> 410 us (0.80)
  waiting for transfers between devices: 453 us -> 4.01 us
  Pallas kernels: 0 us -> 399 us
  other arithmetic: 25 us -> 0 us
  local copies, waits for them, and re-layouts: 21.8 us -> 2.44 us
  between operations: 14.2 us -> 0.67 us
    pallas_call x0 -> x3, Pallas kernels: none -> 399 us  [the longest x1 382 us: step(): pl.pallas_call(lambda *refs: kernel(n, *refs), out_shape=(*(pltpu.VMEM(w....]
    all_gather x3 -> x0, waiting for transfers between devices: 234 us -> none  [step(): whole = [lax.all_gather(one[0], 'dp', axis=1, tiled=True) for one in new]]
    reduce_scatter x3 -> x0, waiting for transfers between devices: 217 us -> none  [step(): lax.psum_scatter(t[0], 'dp', scatter_dimension=1, tiled=True)]
    convert_element_type x3 -> x0, other arithmetic: 25 us -> none  [adamw(): return ((w - 0.02 * step).astype(jnp.bfloat16), m, v)]
    unnamed x3 -> x4, local copies, waits for them, and re-layouts: 21.8 us -> 2.44 us
  transfers between devices with their start and end apart: 6 -> 2, of which waited for: 6 -> 1; matrix products, arithmetic and copies ran while one was open for 5% -> 0% of each run, Pallas kernels for 0% -> 4%
where the time goes in v3:
time: 410 us; the launch traced here: 409 us
  Pallas kernels  399 us (97%)
    pallas_call x1, Pallas kernels, step(): pl.pallas_call(lambda *refs: kernel(n, *refs), out_shape=(*(pltpu.VMEM(w....  382 us
    pallas_call x1, Pallas kernels, unload(): pl.pallas_call(lambda *refs: unload_kernel(n, *refs), out_shape=[jax.Shap...  15.3 us
  transfers between devices with their start and end apart: 2, of which 1 were waited for; matrix products, arithmetic and copies ran while one was open for 0% of the time, Pallas kernels for 4%

profile of v3, /device:TPU:112, one launch (start us, length us, event | category | flops | bytes accessed | tf_op | source)
XLA Modules:
  0.0 409.0 jit_solution(251834975558216552)
XLA Ops:
  0.6 381.9 %sharded_adamw.1 = (bf16[2,896,2304]{2,1,0:T(8,128)(2,1)S(1)}, bf16[2,896,2304]{2,1,0:T(8,128)(2,1)S(1)}, bf16[2,2304,896]{2,1,0:T(8,128)(2,1)S(1)}, f32[2,224,2...) custom-call(bf16[1,2,896,2304]{3,2,1,0:T(8,128)(2,1)} %refs_0_.1, ...), custom_call_target="tpu_custom_call" | custom-call | tf_op jit(solution)/shard_map/sharded_adamw/pallas_call | solution.py:233
  382.6 1.4 collective-permute-start
  384.0 1.9 collective-permute-start.1
  385.9 0.0 copy-start
  385.9 1.2 copy-done
  387.1 0.0 copy-start.1
  387.1 1.2 copy-done.1
  388.3 15.3 %unload.1 = (bf16[2,896,2304]{2,1,0:T(8,128)(2,1)}, bf16[2,896,2304]{2,1,0:T(8,128)(2,1)}, bf16[2,2304,896]{2,1,0:T(8,128)(2,1)}, f32[2,224,2304]{2,1,0:T(8,128)...) custom-call(bf16[2,288,896]{2,1,0:T(8,128)(2,1)S(1)} %copy-done.1, ...), custom_call_target="tpu_custom_call" | custom-call | flops 3170893824 | bytes 49545216 | tf_op jit(solution)/shard_map/unload/pallas_call | solution.py:189
  403.6 4.0 collective-permute-done.refs_0_
  407.6 0.0 collective-permute-done.1.refs_1_
  407.6 1.3 finish.1
Async XLA Ops:
  382.6 25.1 %collective-permute-start = (bf16[2,288,896]{2,1,0:T(8,128)(2,1)}, bf16[2,288,896]{2,1,0:T(8,128)(2,1)S(1)}, u32[]{:S(2)}, u32[]{:S(2)}) collective-permute-start(bf16[2,288,896]{2,1,0:T(8,128)(2,1)} %get-tuple-element.29.refs_0_), channel_id=1, source_target_pairs={{0,1},{1,2},{2,3},{3,0},{4,5},{5,6},{6,7},{7,4},{8,9},{9,10},{10,1... | collective-permute-start | bytes 3096584 | tf_op jit(solution)/shard_map/ppermute | solution.py:258
  384.0 23.6 %collective-permute-start.1 = (bf16[2,288,896]{2,1,0:T(8,128)(2,1)}, bf16[2,288,896]{2,1,0:T(8,128)(2,1)S(1)}, u32[]{:S(2)}, u32[]{:S(2)}) collective-permute-start(bf16[2,288,896]{2,1,0:T(8,128)(2,1)} %get-tuple-element.30.refs_1_), channel_id=1, source_target_pairs={{0,3},{1,0},{2,1},{3,2},{4,7},{5,4},{6,5},{7,6},{8,11},{9,8},{10,9... | collective-permute-start | bytes 3096584 | tf_op jit(solution)/shard_map/ppermute | solution.py:258
  385.9 1.2 copy-start
  387.1 1.2 copy-start.1
